TPU v7x, 32 devices: a whole 2x2x4 slice. The times are simulated.
32 devices in a mesh: section: 4 (over z), dom: 8 (over y, x, core).
Axes of the slice: x: 2, y: 2, z: 4, core: 2. Of those that a mesh axis runs over, the one named last changes fastest.
Arguments:
- layer_inputs: bfloat16 [4, 16384, 512], P('section', 'dom'), may hold values from -6 to 6
- adjacency: bfloat16 [128, 8, 128, 128], P('dom'), may hold values from -0.1875 to 0.1875
- columns: int32 [128, 8], P('dom'), may hold values from 0 to 127, as said below
- group_order: int32 [8, 4], P('dom'), may hold values from 0 to 3, each once within a row
- weights: bfloat16 [4, 512, 512], P('section'), may hold values from -0.25 to 0.25
Outputs:
- embeddings: bfloat16 [4, 16384, 512], P('section', 'dom')
Inputs may be any that keep to these rules, and one draw needn't show every extreme that they name: `columns`: the tiles of a row block of part p name row blocks of parts p - 1, p and p + 1, counted modulo 8. `group_order`: each row is a permutation.
All inputs are finite; a program needn't handle non-finite values.
Results may differ from a plain program's by a relative error of at most 0.0095.
Values may be sent and summed in bfloat16 or wider, within the bound.
A program may use at most 64 MiB of HBM per device.

v0:
```python
import functools

import jax
import jax.numpy as jnp
from jax import lax
from jax.experimental import pallas as pl
from jax.experimental.pallas import tpu as pltpu
from jax.sharding import PartitionSpec as P

MESH = pl.DeviceIdType.MESH


def relay_plan(sections, blocks):
    far, near = blocks // 4, blocks // 8
    return ((sections - 1, 0, far), (sections - 2, far, near))


def pipeline_kernel(
    sections, parts, groups, columns, own_order, order_ref, x_ref, adj_hbm, w_ref, out_ref,
    table, position, order_land, near_order, order_send, order_recv, order_local,
    adj, src, mine, own_land, side_land, relay_up, relay_over,
    adj_sem, stale_send, stale_recv, z_send, z_recv, f_send, f_recv,
    up_send, up_recv, over_send, over_recv, down_send, down_recv,
):
    s = lax.axis_index("section")
    d = lax.axis_index("dom")
    right, left = lax.rem(d + 1, parts), lax.rem(d + parts - 1, parts)
    blocks, side, width = x_ref.shape
    tiles = adj.shape[1]
    bg = blocks // groups
    fresh = 3 * blocks
    last = sections - 1
    odd = lax.rem(d, 2)
    across = lax.rem(d + parts - 1 + 2 * odd, parts)
    from_across = jnp.where(odd == 1, 2 * blocks, 0)
    relays = relay_plan(sections, blocks)
    relayed = sum(count for _, _, count in relays)
    direct = blocks - relayed

    load_adj = pltpu.make_async_copy(adj_hbm, adj, adj_sem)
    load_adj.start()

    for k in range(groups):
        piece = x_ref[pl.ds(own_order[0, k] * bg, bg)]
        mine[k * bg:(k + 1) * bg] = piece
        src[blocks + k * bg:blocks + (k + 1) * bg] = piece

    barrier = pltpu.get_barrier_semaphore()
    for neighbour in (left, right):
        pl.semaphore_signal(barrier, inc=1, device_id={"dom": neighbour}, device_id_type=MESH)

    @pl.when(s > 0)
    def _():
        pl.semaphore_signal(barrier, inc=1, device_id={"section": s - 1}, device_id_type=MESH)

    @pl.when(s < last)
    def _():
        pl.semaphore_signal(barrier, inc=1, device_id={"section": s + 1}, device_id_type=MESH)

    peers = 2 + jnp.where(s > 0, 1, 0) + jnp.where(s < last, 1, 0)
    for plane, _, _ in relays:
        peers = peers + jnp.where(s == 0, 1, 0) + jnp.where(s == plane, 1, 0)

        @pl.when(s == 0)
        def _():
            pl.semaphore_signal(barrier, inc=1, device_id={"section": plane}, device_id_type=MESH)

        @pl.when(s == plane)
        def _():
            pl.semaphore_signal(barrier, inc=1, device_id={"section": 0}, device_id_type=MESH)

    pl.semaphore_wait(barrier, peers)

    def order_copy(way):
        return pltpu.make_async_remote_copy(
            src_ref=order_ref,
            dst_ref=order_land.at[way],
            send_sem=order_send.at[way],
            recv_sem=order_recv.at[way],
            device_id={"dom": right if way == 0 else left},
            device_id_type=MESH,
        )

    for way in range(2):
        order_copy(way).start()

    def stale_copy(way, k):
        base = (0 if way == 0 else 2 * blocks) + k * bg
        return pltpu.make_async_remote_copy(
            src_ref=mine.at[pl.ds(k * bg, bg)],
            dst_ref=src.at[pl.ds(base, bg)],
            send_sem=stale_send.at[way, k],
            recv_sem=stale_recv.at[way, k],
            device_id={"dom": right if way == 0 else left},
            device_id_type=MESH,
        )

    def side_copy(way, r):
        return pltpu.make_async_remote_copy(
            src_ref=own_land.at[r],
            dst_ref=side_land.at[way, r],
            send_sem=f_send.at[way, r],
            recv_sem=f_recv.at[way, r],
            device_id={"dom": right if way == 0 else left},
            device_id_type=MESH,
        )

    def up_copy(r):
        return pltpu.make_async_remote_copy(
            src_ref=out_ref.at[r],
            dst_ref=own_land.at[r],
            send_sem=z_send.at[r],
            recv_sem=z_recv.at[r],
            device_id={"section": jnp.minimum(s + 1, last)},
            device_id_type=MESH,
        )

    def partner_copy():
        return pltpu.make_async_remote_copy(
            src_ref=mine,
            dst_ref=src.at[pl.ds(jnp.where(odd == 1, 2 * blocks, 0), blocks)],
            send_sem=stale_send.at[0, 0],
            recv_sem=stale_recv.at[0, 0],
            device_id={"dom": jnp.where(odd == 1, left, right)},
            device_id_type=MESH,
        )

    def across_copy():
        return pltpu.make_async_remote_copy(
            src_ref=mine.at[pl.ds(0, direct)],
            dst_ref=src.at[pl.ds(jnp.where(odd == 1, 0, 2 * blocks), direct)],
            send_sem=stale_send.at[1, 0],
            recv_sem=stale_recv.at[1, 0],
            device_id={"dom": across},
            device_id_type=MESH,
        )

    def relay_up_copy(plane, b):
        return pltpu.make_async_remote_copy(
            src_ref=mine.at[direct + b],
            dst_ref=relay_up.at[b],
            send_sem=up_send.at[b],
            recv_sem=up_recv.at[b],
            device_id={"section": plane},
            device_id_type=MESH,
        )

    def relay_over_copy(b):
        return pltpu.make_async_remote_copy(
            src_ref=relay_up.at[b],
            dst_ref=relay_over.at[b],
            send_sem=over_send.at[b],
            recv_sem=over_recv.at[b],
            device_id={"dom": across},
            device_id_type=MESH,
        )

    def relay_down_copy(b):
        return pltpu.make_async_remote_copy(
            src_ref=relay_over.at[b],
            dst_ref=src.at[from_across + direct + b],
            send_sem=down_send.at[b],
            recv_sem=down_recv.at[b],
            device_id={"section": 0},
            device_id_type=MESH,
        )

    def forward(r):
        up_copy(r).wait_recv()
        side_copy(0, r).start()
        side_copy(1, r).start()

    @pl.when(s == 0)
    def _():
        across_copy().start()
        for plane, first, count in relays:
            @pl.loop(first, first + count)
            def _(b):
                relay_up_copy(plane, b).start()

        partner_copy().start()

    for plane, first, count in relays:
        @pl.when(s == plane)
        def _():
            @pl.loop(first, first + count)
            def _(b):
                relay_up_copy(plane, b).wait_recv()
                relay_over_copy(b).start()

            for k in range(1, groups):
                for way in range(2):
                    stale_copy(way, k).start()

            @pl.loop(first, first + count)
            def _(b):
                relay_over_copy(b).wait_recv()
                relay_down_copy(b).start()

    plain = s > 0
    for plane, _, _ in relays:
        plain = plain & (s != plane)

    @pl.when(plain)
    def _():
        for k in range(1, groups):
            for way in range(2):
                stale_copy(way, k).start()

    for way in range(2):
        order_copy(way).wait()
        local = pltpu.make_async_copy(
            order_land.at[way], near_order.at[way], order_local.at[way]
        )
        local.start()
        local.wait()

    for p in range(3):
        for g in range(groups):
            step = jnp.int32(0)
            for k in range(1, groups):
                held = own_order[0, k] if p == 1 else near_order[p // 2, 0, k]
                step = jnp.where(held == g, k, step)
            position[p * groups + g] = step

    later = s > 0

    @pl.loop(0, blocks)
    def _(r):
        k = r // bg
        row = own_order[0, k] * bg + r % bg
        for t in range(tiles):
            column = columns[row, t]
            relative = jnp.minimum(lax.rem(lax.div(column, blocks) - d + 1 + parts, parts), 2)
            inside = lax.rem(column, blocks)
            step = position[relative * groups + lax.div(inside, bg)]
            slot = relative * blocks + step * bg + lax.rem(inside, bg)
            table[r * tiles + t] = slot + jnp.where(later & (step <= k), fresh, 0)

    load_adj.wait()
    own_base = jnp.where(s > 0, fresh + blocks, blocks)

    for k in range(groups):
        lo, hi = k * bg, (k + 1) * bg

        @pl.when(s > 0)
        def _():
            if k == 0:
                @pl.loop(lo, hi)
                def _(r):
                    forward(r)

            src[fresh + blocks + lo:fresh + blocks + hi] = own_land[lo:hi]

            @pl.loop(lo, hi)
            def _(r):
                side_copy(0, r).wait_recv()
                side_copy(1, r).wait_recv()

            src[fresh + lo:fresh + hi] = side_land[0, lo:hi]
            src[fresh + 2 * blocks + lo:fresh + 2 * blocks + hi] = side_land[1, lo:hi]

        if k == 0:
            @pl.when(s == 0)
            def _():
                partner_copy().wait_recv()
                across_copy().wait_recv()

                @pl.loop(0, relayed)
                def _(b):
                    relay_down_copy(b).wait_recv()

            @pl.when(s > 0)
            def _():
                for q in range(1, groups):
                    for way in range(2):
                        stale_copy(way, q).wait_recv()

        @pl.loop(lo, hi)
        def _(r):
            if k + 1 < groups:
                @pl.when(s > 0)
                def _():
                    forward(r + bg)

            row = own_order[0, k] * bg + (r - lo)
            a = jnp.concatenate([adj[row, t] for t in range(tiles)], axis=1)
            h = jnp.concatenate([src[table[r * tiles + t]] for t in range(tiles)], axis=0)
            agg = jnp.dot(a, h, preferred_element_type=jnp.float32).astype(jnp.bfloat16)
            product = jnp.dot(agg, w_ref[...], preferred_element_type=jnp.float32)
            before = src[own_base + r].astype(jnp.float32)
            out_ref[r] = (before + jnp.maximum(product, 0.0)).astype(jnp.bfloat16)

            @pl.when(s < last)
            def _():
                up_copy(r).start()

    @pl.when(s == 0)
    def _():
        partner_copy().wait_send()
        across_copy().wait_send()
        for plane, first, count in relays:
            @pl.loop(first, first + count)
            def _(b):
                relay_up_copy(plane, b).wait_send()

    for plane, first, count in relays:
        @pl.when(s == plane)
        def _():
            @pl.loop(first, first + count)
            def _(b):
                relay_over_copy(b).wait_send()
                relay_down_copy(b).wait_send()

    @pl.when(s > 0)
    def _():
        for k in range(1, groups):
            for way in range(2):
                stale_copy(way, k).wait_send()

        @pl.loop(0, blocks)
        def _(r):
            side_copy(0, r).wait_send()
            side_copy(1, r).wait_send()

    @pl.when(s < last)
    def _():
        @pl.loop(0, blocks)
        def _(r):
            up_copy(r).wait_send()


def place_kernel(groups, order, h_hbm, out_hbm, held, in_sem, out_sem):
    bg = h_hbm.shape[0] // groups

    def load(k):
        rows = pl.ds(k * bg, bg)
        return pltpu.make_async_copy(h_hbm.at[rows], held.at[rows], in_sem.at[k])

    def store(k):
        return pltpu.make_async_copy(
            held.at[pl.ds(k * bg, bg)], out_hbm.at[pl.ds(order[k] * bg, bg)], out_sem.at[k]
        )

    for k in range(groups):
        load(k).start()
    for k in range(groups):
        load(k).wait()
        store(k).start()
    for k in range(groups):
        store(k).wait()


def on_device(sections, layer_inputs, adjacency, columns, group_order, weights):
    parts = lax.axis_size("dom")
    rows, width = layer_inputs.shape[1:]
    blocks, tiles, side = adjacency.shape[:3]
    groups = group_order.shape[1]
    relayed = sum(count for _, _, count in relay_plan(sections, blocks))
    dma = pltpu.SemaphoreType.DMA
    hidden = pl.pallas_call(
        functools.partial(pipeline_kernel, sections, parts, groups),
        out_shape=jax.ShapeDtypeStruct((blocks, side, width), jnp.bfloat16),
        in_specs=[
            pl.BlockSpec(memory_space=pltpu.SMEM),
            pl.BlockSpec(memory_space=pltpu.SMEM),
            pl.BlockSpec(memory_space=pltpu.VMEM),
            pl.BlockSpec(memory_space=pltpu.VMEM),
            pl.BlockSpec(memory_space=pl.ANY),
            pl.BlockSpec(memory_space=pltpu.VMEM),
        ],
        out_specs=pl.BlockSpec(memory_space=pltpu.VMEM),
        scratch_shapes=[
            pltpu.SMEM((blocks * tiles,), jnp.int32),
            pltpu.SMEM((3 * groups,), jnp.int32),
            pltpu.VMEM((2, 1, groups), jnp.int32),
            pltpu.SMEM((2, 1, groups), jnp.int32),
            dma((2,)),
            dma((2,)),
            dma((2,)),
            pltpu.VMEM(adjacency.shape, jnp.bfloat16),
            pltpu.VMEM((6 * blocks, side, width), jnp.bfloat16),
            pltpu.VMEM((blocks, side, width), jnp.bfloat16),
            pltpu.VMEM((blocks, side, width), jnp.bfloat16),
            pltpu.VMEM((2, blocks, side, width), jnp.bfloat16),
            pltpu.VMEM((relayed, side, width), jnp.bfloat16),
            pltpu.VMEM((relayed, side, width), jnp.bfloat16),
            dma,
            dma((2, groups)),
            dma((2, groups)),
            dma((blocks,)),
            dma((blocks,)),
            dma((2, blocks)),
            dma((2, blocks)),
        ] + [dma((relayed,))] * 6,
        compiler_params=pltpu.CompilerParams(
            collective_id=0, has_side_effects=True, vmem_limit_bytes=56 * 2**20
        ),
    )(
        columns, group_order, group_order,
        layer_inputs.reshape(blocks, side, width), adjacency, weights[0],
    )

    placed = pl.pallas_call(
        functools.partial(place_kernel, groups),
        out_shape=jax.ShapeDtypeStruct((blocks, side, width), jnp.bfloat16),
        in_specs=[
            pl.BlockSpec(memory_space=pltpu.SMEM),
            pl.BlockSpec(memory_space=pl.ANY),
        ],
        out_specs=pl.BlockSpec(memory_space=pl.ANY),
        scratch_shapes=[
            pltpu.VMEM((blocks, side, width), jnp.bfloat16), dma((groups,)), dma((groups,)),
        ],
    )(group_order[0], hidden)
    return placed.reshape(1, rows, width)


def solution(mesh):
    in_specs = (
        P("section", "dom", None),
        P("dom", None, None, None),
        P("dom", None),
        P("dom", None),
        P("section", None, None),
    )
    return jax.shard_map(
        functools.partial(on_device, mesh.shape["section"]),
        mesh=mesh, in_specs=in_specs, out_specs=P("section", "dom", None), check_vma=False,
    )
```

profile of v0, /device:TPU:27, one launch (start us, length us, event | category | flops | bytes accessed | tf_op | source)
XLA Modules:
  0.0 140.6 jit_solution(17162469724565724654)
XLA Ops:
  0.0 1.4 copy.6.columns
  1.4 136.1 %shard_map.55.h_hbm = bf16[16,128,512]{2,1,0:T(8,128)(2,1)} custom-call(s32[16,8]{1,0:T(8,128)} %copy.6.columns, s32[1,4]{1,0:T(1,128)} %order_ref.1, s32[1,4]{1,0:T(1,128)} %order_ref.1, bf16[16,128,512]{2,1,0:T(8,128)(2,1)} %bitcast.4, bf16[16,8,128,128]{3,2,1,0:T(8,128)(2,1)} %adj_hbm.1, bf16[512,512]{1,0:T(8,128)(2,1)} %bitcast.5), custom_call_target="tpu_custom_call" | custom-call | tf_op jit(solution)/shard_map/pallas_call | solution.py:361
  137.5 3.1 %shard_map.56 = bf16[16,128,512]{2,1,0:T(8,128)(2,1)} custom-call(s32[4]{0:T(128)} %bitcast.6, bf16[16,128,512]{2,1,0:T(8,128)(2,1)} %shard_map.55.h_hbm), custom_call_target="tpu_custom_call" | custom-call | tf_op jit(solution)/shard_map/pallas_call | solution.py:404
where the time goes:
time: 142 us; the launch traced here: 141 us
  Pallas kernels  139 us (98%)
    pallas_call x1, Pallas kernels, on_device(): pl.pallas_call(functools.partial(pipeline_kernel, sections, parts, groups...  136 us
    pallas_call x1, Pallas kernels, on_device(): pl.pallas_call(functools.partial(place_kernel, groups), out_shape=jax.Sha...  3.09 us

commit v1 on v0

v1 whole, which is shorter than its diff:
```python
import functools

import jax
import jax.numpy as jnp
from jax import lax
from jax.experimental import pallas as pl
from jax.experimental.pallas import tpu as pltpu
from jax.sharding import PartitionSpec as P

MESH = pl.DeviceIdType.MESH
SPLIT = 2
AHEAD = 2


def relay_counts(blocks):
    return blocks * 7 // 16, blocks // 8


def pipeline_kernel(
    sections, parts, groups, columns, own_order, order_ref, x_ref, adj_hbm, w_ref, out_ref,
    table, position, order_land, near_order, order_send, order_recv, order_local,
    adj, src, mine, own_land, side_land, first_land, stored_land,
    adj_sem, partner_send, partner_recv, across_send, across_recv, z_send, z_recv, f_send, f_recv,
    over_send, over_recv, down_send, down_recv, sover_send, sover_recv, sdown_send, sdown_recv,
):
    s = lax.axis_index("section")
    d = lax.axis_index("dom")
    right, left = lax.rem(d + 1, parts), lax.rem(d + parts - 1, parts)
    blocks, side, width = x_ref.shape
    tiles = adj.shape[1]
    bg = blocks // groups
    fresh = 3 * blocks
    last = sections - 1
    odd = lax.rem(d, 2)
    partner = jnp.where(odd == 1, left, right)
    across = jnp.where(odd == 1, right, left)
    to_partner = jnp.where(odd == 1, 2 * blocks, 0)
    to_across = jnp.where(odd == 1, 0, 2 * blocks)
    from_across = jnp.where(odd == 1, 2 * blocks, 0)
    relayed, stored = relay_counts(blocks)
    direct = blocks - relayed
    low, mid = 1, 2
    half = side // SPLIT
    per_group = bg * SPLIT

    load_adj = pltpu.make_async_copy(adj_hbm, adj, adj_sem)
    load_adj.start()

    for k in range(groups):
        piece = x_ref[pl.ds(own_order[0, k] * bg, bg)]
        mine[k * bg:(k + 1) * bg] = piece
        src[blocks + k * bg:blocks + (k + 1) * bg] = piece

    barrier = pltpu.get_barrier_semaphore()

    def greet(there):
        pl.semaphore_signal(barrier, inc=1, device_id=there, device_id_type=MESH)

    peers = 2
    for neighbour in (left, right):
        greet({"dom": neighbour})
    for mask, there in (
        (s > 0, {"section": jnp.maximum(s - 1, 0)}),
        (s < last, {"section": jnp.minimum(s + 1, last)}),
        (s == 0, {"section": last, "dom": across}),
        (s == last, {"section": 0, "dom": across}),
        (s == 0, {"section": last}),
        (s == last, {"section": 0}),
        (s == low, {"section": mid, "dom": across}),
        (s == mid, {"section": low, "dom": across}),
    ):
        peers = peers + jnp.where(mask, 1, 0)

        @pl.when(mask)
        def _():
            greet(there)

    pl.semaphore_wait(barrier, peers)

    def order_copy(way):
        return pltpu.make_async_remote_copy(
            src_ref=order_ref,
            dst_ref=order_land.at[way],
            send_sem=order_send.at[way],
            recv_sem=order_recv.at[way],
            device_id={"dom": right if way == 0 else left},
            device_id_type=MESH,
        )

    def partner_copy(first, count):
        return pltpu.make_async_remote_copy(
            src_ref=mine.at[pl.ds(first, count)],
            dst_ref=src.at[pl.ds(to_partner + first, count)],
            send_sem=partner_send,
            recv_sem=partner_recv,
            device_id={"dom": partner},
            device_id_type=MESH,
        )

    def across_copy(n, first, count):
        return pltpu.make_async_remote_copy(
            src_ref=mine.at[pl.ds(first, count)],
            dst_ref=src.at[pl.ds(to_across + first, count)],
            send_sem=across_send.at[n],
            recv_sem=across_recv.at[n],
            device_id={"dom": across},
            device_id_type=MESH,
        )

    def over_copy(b):
        return pltpu.make_async_remote_copy(
            src_ref=mine.at[direct + b],
            dst_ref=first_land.at[b],
            send_sem=over_send.at[b],
            recv_sem=over_recv.at[b],
            device_id={"section": last, "dom": across},
            device_id_type=MESH,
        )

    def down_copy(b):
        return pltpu.make_async_remote_copy(
            src_ref=first_land.at[b],
            dst_ref=src.at[from_across + direct + b],
            send_sem=down_send.at[b],
            recv_sem=down_recv.at[b],
            device_id={"section": 0},
            device_id_type=MESH,
        )

    def stored_over_copy(b):
        return pltpu.make_async_remote_copy(
            src_ref=mine.at[blocks - stored + b],
            dst_ref=stored_land.at[b],
            send_sem=sover_send.at[b],
            recv_sem=sover_recv.at[b],
            device_id={"section": mid, "dom": across},
            device_id_type=MESH,
        )

    def stored_down_copy(b):
        return pltpu.make_async_remote_copy(
            src_ref=stored_land.at[b],
            dst_ref=src.at[from_across + blocks - stored + b],
            send_sem=sdown_send.at[b],
            recv_sem=sdown_recv.at[b],
            device_id={"section": low},
            device_id_type=MESH,
        )

    def up_copy(r, h):
        q = r * SPLIT + h
        return pltpu.make_async_remote_copy(
            src_ref=out_ref.at[r, pl.ds(h * half, half)],
            dst_ref=own_land.at[q],
            send_sem=z_send.at[q],
            recv_sem=z_recv.at[q],
            device_id={"section": jnp.minimum(s + 1, last)},
            device_id_type=MESH,
        )

    def up_wait(q):
        pltpu.make_async_remote_copy(
            src_ref=own_land.at[q],
            dst_ref=own_land.at[q],
            send_sem=z_send.at[q],
            recv_sem=z_recv.at[q],
            device_id={"section": jnp.minimum(s + 1, last)},
            device_id_type=MESH,
        ).wait_recv()

    def side_copy(way, q):
        return pltpu.make_async_remote_copy(
            src_ref=own_land.at[q],
            dst_ref=side_land.at[way, q],
            send_sem=f_send.at[way, q],
            recv_sem=f_recv.at[way, q],
            device_id={"dom": right if way == 0 else left},
            device_id_type=MESH,
        )

    def forward(q):
        up_wait(q)
        side_copy(0, q).start()
        side_copy(1, q).start()

    def stale_pieces(kept):
        return [(0, bg, bg), (1, 2 * bg, bg), (2, 3 * bg, bg - kept)]

    for way in range(2):
        order_copy(way).start()

    @pl.when(s == 0)
    def _():
        @pl.loop(0, relayed)
        def _(b):
            over_copy(b).start()

        across_copy(0, 0, direct).start()
        partner_copy(0, blocks).start()

    @pl.when(s == last)
    def _():
        @pl.loop(0, relayed)
        def _(b):
            over_copy(b).wait_recv()
            down_copy(b).start()

    @pl.when(s == low)
    def _():
        for n, first, count in stale_pieces(stored):
            across_copy(n, first, count).start()

    @pl.when(s > low)
    def _():
        for n, first, count in stale_pieces(0):
            across_copy(n, first, count).start()

    @pl.when(s > 0)
    def _():
        partner_copy(bg, blocks - bg).start()

    for way in range(2):
        order_copy(way).wait()
        local = pltpu.make_async_copy(
            order_land.at[way], near_order.at[way], order_local.at[way]
        )
        local.start()
        local.wait()

    for p in range(3):
        for g in range(groups):
            step = jnp.int32(0)
            for k in range(1, groups):
                held = own_order[0, k] if p == 1 else near_order[p // 2, 0, k]
                step = jnp.where(held == g, k, step)
            position[p * groups + g] = step

    later = s > 0

    @pl.loop(0, blocks)
    def _(r):
        k = r // bg
        row = own_order[0, k] * bg + r % bg
        for t in range(tiles):
            column = columns[t, row]
            relative = jnp.minimum(lax.rem(lax.div(column, blocks) - d + 1 + parts, parts), 2)
            inside = lax.rem(column, blocks)
            step = position[relative * groups + lax.div(inside, bg)]
            slot = relative * blocks + step * bg + lax.rem(inside, bg)
            table[r * tiles + t] = slot + jnp.where(later & (step <= k), fresh, 0)

    load_adj.wait()
    own_base = jnp.where(s > 0, fresh + blocks, blocks)

    @pl.when(s == low)
    def _():
        for n, first, count in stale_pieces(stored)[:2]:
            across_copy(n, first, count).wait_recv()

        @pl.loop(0, stored)
        def _(b):
            stored_over_copy(b).start()

    @pl.when(s == mid)
    def _():
        @pl.loop(0, stored)
        def _(b):
            stored_over_copy(b).wait_recv()
            stored_down_copy(b).start()

    for k in range(groups):
        lo, hi = k * bg, (k + 1) * bg
        plo, phi = lo * SPLIT, hi * SPLIT

        @pl.when(s > 0)
        def _():
            if k == 0:
                @pl.loop(0, per_group + AHEAD)
                def _(q):
                    forward(q)

            def as_blocks(pieces):
                return pieces.reshape(bg, side, width)

            src[fresh + blocks + lo:fresh + blocks + hi] = as_blocks(own_land[plo:phi])

            @pl.loop(plo, phi)
            def _(q):
                side_copy(0, q).wait_recv()
                side_copy(1, q).wait_recv()

            src[fresh + lo:fresh + hi] = as_blocks(side_land[0, plo:phi])
            src[fresh + 2 * blocks + lo:fresh + 2 * blocks + hi] = as_blocks(side_land[1, plo:phi])

        if k == 0:
            @pl.when(s == 0)
            def _():
                partner_copy(0, blocks).wait_recv()
                across_copy(0, 0, direct).wait_recv()

                @pl.loop(0, relayed)
                def _(b):
                    down_copy(b).wait_recv()

            @pl.when(s > 0)
            def _():
                partner_copy(bg, blocks - bg).wait_recv()

            @pl.when(s == low)
            def _():
                across_copy(*stale_pieces(stored)[2]).wait_recv()

                @pl.loop(0, stored)
                def _(b):
                    stored_down_copy(b).wait_recv()

            @pl.when(s > low)
            def _():
                for n, first, count in stale_pieces(0):
                    across_copy(n, first, count).wait_recv()

        @pl.loop(lo, hi)
        def _(r):
            row = own_order[0, k] * bg + (r - lo)
            a = jnp.concatenate([adj[row, t] for t in range(tiles)], axis=1)
            h = jnp.concatenate([src[table[r * tiles + t]] for t in range(tiles)], axis=0)
            agg = jnp.dot(a, h, preferred_element_type=jnp.float32).astype(jnp.bfloat16)
            product = jnp.dot(agg, w_ref[...], preferred_element_type=jnp.float32)
            before = src[own_base + r].astype(jnp.float32)
            out_ref[r] = (before + jnp.maximum(product, 0.0)).astype(jnp.bfloat16)

            @pl.when(s < last)
            def _():
                for h_ in range(SPLIT):
                    up_copy(r, h_).start()

            if k + 1 < groups:
                @pl.when(s > 0)
                def _():
                    forward(phi + AHEAD + (r - lo))

        if k + 1 < groups:
            more = per_group + (AHEAD if k + 2 < groups else 0)

            @pl.when(s > 0)
            def _():
                @pl.loop(phi + AHEAD + bg, phi + more)
                def _(q):
                    forward(q)

    @pl.when(s == 0)
    def _():
        partner_copy(0, blocks).wait_send()
        across_copy(0, 0, direct).wait_send()

        @pl.loop(0, relayed)
        def _(b):
            over_copy(b).wait_send()

    @pl.when(s == last)
    def _():
        @pl.loop(0, relayed)
        def _(b):
            down_copy(b).wait_send()

    @pl.when(s == low)
    def _():
        for n, first, count in stale_pieces(stored):
            across_copy(n, first, count).wait_send()

        @pl.loop(0, stored)
        def _(b):
            stored_over_copy(b).wait_send()

    @pl.when(s == mid)
    def _():
        @pl.loop(0, stored)
        def _(b):
            stored_down_copy(b).wait_send()

    @pl.when(s > low)
    def _():
        for n, first, count in stale_pieces(0):
            across_copy(n, first, count).wait_send()

    @pl.when(s > 0)
    def _():
        partner_copy(bg, blocks - bg).wait_send()

        @pl.loop(0, blocks * SPLIT)
        def _(q):
            side_copy(0, q).wait_send()
            side_copy(1, q).wait_send()

    @pl.when(s < last)
    def _():
        @pl.loop(0, blocks)
        def _(r):
            for h_ in range(SPLIT):
                up_copy(r, h_).wait_send()


def place_kernel(groups, order, h_hbm, out_hbm, held, in_sem, out_sem):
    bg = h_hbm.shape[0] // groups

    def load(k):
        rows = pl.ds(k * bg, bg)
        return pltpu.make_async_copy(h_hbm.at[rows], held.at[rows], in_sem.at[k])

    def store(k):
        return pltpu.make_async_copy(
            held.at[pl.ds(k * bg, bg)], out_hbm.at[pl.ds(order[k] * bg, bg)], out_sem.at[k]
        )

    for k in range(groups):
        load(k).start()
    for k in range(groups):
        load(k).wait()
        store(k).start()
    for k in range(groups):
        store(k).wait()


def on_device(sections, layer_inputs, adjacency, columns, group_order, weights):
    parts = lax.axis_size("dom")
    rows, width = layer_inputs.shape[1:]
    blocks, tiles, side = adjacency.shape[:3]
    groups = group_order.shape[1]
    relayed, stored = relay_counts(blocks)
    pieces = blocks * SPLIT
    dma = pltpu.SemaphoreType.DMA
    hidden = pl.pallas_call(
        functools.partial(pipeline_kernel, sections, parts, groups),
        out_shape=jax.ShapeDtypeStruct((blocks, side, width), jnp.bfloat16),
        in_specs=[
            pl.BlockSpec(memory_space=pltpu.SMEM),
            pl.BlockSpec(memory_space=pltpu.SMEM),
            pl.BlockSpec(memory_space=pltpu.VMEM),
            pl.BlockSpec(memory_space=pltpu.VMEM),
            pl.BlockSpec(memory_space=pl.ANY),
            pl.BlockSpec(memory_space=pltpu.VMEM),
        ],
        out_specs=pl.BlockSpec(memory_space=pltpu.VMEM),
        scratch_shapes=[
            pltpu.SMEM((blocks * tiles,), jnp.int32),
            pltpu.SMEM((3 * groups,), jnp.int32),
            pltpu.VMEM((2, 1, groups), jnp.int32),
            pltpu.SMEM((2, 1, groups), jnp.int32),
            dma((2,)),
            dma((2,)),
            dma((2,)),
            pltpu.VMEM(adjacency.shape, jnp.bfloat16),
            pltpu.VMEM((6 * blocks, side, width), jnp.bfloat16),
            pltpu.VMEM((blocks, side, width), jnp.bfloat16),
            pltpu.VMEM((pieces, side // SPLIT, width), jnp.bfloat16),
            pltpu.VMEM((2, pieces, side // SPLIT, width), jnp.bfloat16),
            pltpu.VMEM((relayed, side, width), jnp.bfloat16),
            pltpu.VMEM((stored, side, width), jnp.bfloat16),
            dma,
            dma,
            dma,
            dma((3,)),
            dma((3,)),
            dma((pieces,)),
            dma((pieces,)),
            dma((2, pieces)),
            dma((2, pieces)),
        ] + [dma((relayed,))] * 4 + [dma((stored,))] * 4,
        compiler_params=pltpu.CompilerParams(
            collective_id=0, has_side_effects=True, vmem_limit_bytes=56 * 2**20
        ),
    )(
        columns.T, group_order, group_order,
        layer_inputs.reshape(blocks, side, width), adjacency, weights[0],
    )

    placed = pl.pallas_call(
        functools.partial(place_kernel, groups),
        out_shape=jax.ShapeDtypeStruct((blocks, side, width), jnp.bfloat16),
        in_specs=[
            pl.BlockSpec(memory_space=pltpu.SMEM),
            pl.BlockSpec(memory_space=pl.ANY),
        ],
        out_specs=pl.BlockSpec(memory_space=pl.ANY),
        scratch_shapes=[
            pltpu.VMEM((blocks, side, width), jnp.bfloat16), dma((groups,)), dma((groups,)),
        ],
    )(group_order[0], hidden)
    return placed.reshape(1, rows, width)


def solution(mesh):
    in_specs = (
        P("section", "dom", None),
        P("dom", None, None, None),
        P("dom", None),
        P("dom", None),
        P("section", None, None),
    )
    return jax.shard_map(
        functools.partial(on_device, mesh.shape["section"]),
        mesh=mesh, in_specs=in_specs, out_specs=P("section", "dom", None), check_vma=False,
    )
```

time: 142 us -> 130 us (0.915)
  Pallas kernels: 139 us -> 130 us
    pallas_call x1, Pallas kernels: 136 us -> 127 us  [on_device(): pl.pallas_call(functools.partial(pipeline_kernel, sections, parts, groups...]
where the time goes in v1:
time: 130 us
  Pallas kernels  130 us (100%)
    pallas_call x1, Pallas kernels, on_device(): pl.pallas_call(functools.partial(pipeline_kernel, sections, parts, groups...  127 us
    pallas_call x1, Pallas kernels, on_device(): pl.pallas_call(functools.partial(place_kernel, groups), out_shape=jax.Sha...  3.09 us

profile of v1, /device:TPU:27, one launch (start us, length us, event | category | flops | bytes accessed | tf_op | source)
XLA Modules:
  0.0 129.8 jit_solution(14267664831428469975)
XLA Ops:
  0.0 126.7 %shard_map.55.h_hbm = bf16[16,128,512]{2,1,0:T(8,128)(2,1)} custom-call(s32[8,16]{1,0:T(8,128)} %bitcast.8, s32[1,4]{1,0:T(1,128)} %order_ref.1, s32[1,4]{1,0:T(1,128)} %order_ref.1, bf16[16,128,512]{2,1,0:T(8,128)(2,1)} %bitcast.5, bf16[16,8,128,128]{3,2,1,0:T(8,128)(2,1)} %adj_hbm.1, bf16[512,512]{1,0:T(8,128)(2,1)} %bitcast.6), custom_call_target="tpu_custom_call" | custom-call | tf_op jit(solution)/shard_map/pallas_call | solution.py:432
  126.7 3.1 %shard_map.56 = bf16[16,128,512]{2,1,0:T(8,128)(2,1)} custom-call(s32[4]{0:T(128)} %bitcast.7, bf16[16,128,512]{2,1,0:T(8,128)(2,1)} %shard_map.55.h_hbm), custom_call_target="tpu_custom_call" | custom-call | tf_op jit(solution)/shard_map/pallas_call | solution.py:477

commit v2 on v1

--- a/solution.py
+++ b/solution.py
@@ -17,8 +17,8 @@
 
 
 def pipeline_kernel(
-    sections, parts, groups, columns, own_order, order_ref, x_ref, adj_hbm, w_ref, out_ref,
-    table, position, order_land, near_order, order_send, order_recv, order_local,
+    sections, parts, groups, columns_hbm, order_hbm, x_hbm, adj_hbm, w_hbm, out_ref,
+    columns, own_order, order_ref, x_ref, w_ref, in_sem, table, position, order_land, near_order, order_send, order_recv, order_local,
     adj, src, mine, own_land, side_land, first_land, stored_land,
     adj_sem, partner_send, partner_recv, across_send, across_recv, z_send, z_recv, f_send, f_recv,
     over_send, over_recv, down_send, down_recv, sover_send, sover_recv, sdown_send, sdown_recv,
@@ -44,7 +44,18 @@
     per_group = bg * SPLIT
 
     load_adj = pltpu.make_async_copy(adj_hbm, adj, adj_sem)
+    loads = [
+        pltpu.make_async_copy(there, here, in_sem.at[n])
+        for n, (there, here) in enumerate((
+            (order_hbm, own_order), (x_hbm, x_ref), (order_hbm, order_ref),
+            (columns_hbm, columns), (w_hbm, w_ref),
+        ))
+    ]
+    for load in loads:
+        load.start()
     load_adj.start()
+    loads[0].wait()
+    loads[1].wait()
 
     for k in range(groups):
         piece = x_ref[pl.ds(own_order[0, k] * bg, bg)]
@@ -186,6 +197,7 @@
     def stale_pieces(kept):
         return [(0, bg, bg), (1, 2 * bg, bg), (2, 3 * bg, bg - kept)]
 
+    loads[2].wait()
     for way in range(2):
         order_copy(way).start()
 
@@ -236,6 +248,7 @@
             position[p * groups + g] = step
 
     later = s > 0
+    loads[3].wait()
 
     @pl.loop(0, blocks)
     def _(r):
@@ -250,6 +263,7 @@
             table[r * tiles + t] = slot + jnp.where(later & (step <= k), fresh, 0)
 
     load_adj.wait()
+    loads[4].wait()
     own_base = jnp.where(s > 0, fresh + blocks, blocks)
 
     @pl.when(s == low)
@@ -400,22 +414,15 @@
                 up_copy(r, h_).wait_send()
 
 
-def place_kernel(groups, order, h_hbm, out_hbm, held, in_sem, out_sem):
-    bg = h_hbm.shape[0] // groups
-
-    def load(k):
-        rows = pl.ds(k * bg, bg)
-        return pltpu.make_async_copy(h_hbm.at[rows], held.at[rows], in_sem.at[k])
+def place_kernel(groups, order, h_ref, out_hbm, out_sem):
+    bg = h_ref.shape[0] // groups
 
     def store(k):
         return pltpu.make_async_copy(
-            held.at[pl.ds(k * bg, bg)], out_hbm.at[pl.ds(order[k] * bg, bg)], out_sem.at[k]
+            h_ref.at[pl.ds(k * bg, bg)], out_hbm.at[pl.ds(order[k] * bg, bg)], out_sem.at[k]
         )
 
     for k in range(groups):
-        load(k).start()
-    for k in range(groups):
-        load(k).wait()
         store(k).start()
     for k in range(groups):
         store(k).wait()
@@ -433,15 +440,16 @@
         functools.partial(pipeline_kernel, sections, parts, groups),
         out_shape=jax.ShapeDtypeStruct((blocks, side, width), jnp.bfloat16),
         in_specs=[
-            pl.BlockSpec(memory_space=pltpu.SMEM),
-            pl.BlockSpec(memory_space=pltpu.SMEM),
-            pl.BlockSpec(memory_space=pltpu.VMEM),
-            pl.BlockSpec(memory_space=pltpu.VMEM),
-            pl.BlockSpec(memory_space=pl.ANY),
-            pl.BlockSpec(memory_space=pltpu.VMEM),
+            pl.BlockSpec(memory_space=pltpu.HBM) for _ in range(5)
         ],
         out_specs=pl.BlockSpec(memory_space=pltpu.VMEM),
         scratch_shapes=[
+            pltpu.SMEM((tiles, blocks), jnp.int32),
+            pltpu.SMEM((1, groups), jnp.int32),
+            pltpu.VMEM((1, groups), jnp.int32),
+            pltpu.VMEM((blocks, side, width), jnp.bfloat16),
+            pltpu.VMEM((width, width), jnp.bfloat16),
+            dma((5,)),
             pltpu.SMEM((blocks * tiles,), jnp.int32),
             pltpu.SMEM((3 * groups,), jnp.int32),
             pltpu.VMEM((2, 1, groups), jnp.int32),
@@ -467,11 +475,13 @@
             dma((2, pieces)),
         ] + [dma((relayed,))] * 4 + [dma((stored,))] * 4,
         compiler_params=pltpu.CompilerParams(
-            collective_id=0, has_side_effects=True, vmem_limit_bytes=56 * 2**20
+            collective_id=0, has_side_effects=True, vmem_limit_bytes=50 * 2**20
         ),
     )(
-        columns.T, group_order, group_order,
-        layer_inputs.reshape(blocks, side, width), adjacency, weights[0],
+        *(pltpu.with_memory_space_constraint(array, pltpu.HBM) for array in (
+            columns.T, group_order, layer_inputs.reshape(blocks, side, width),
+            adjacency, weights[0],
+        ))
     )
 
     placed = pl.pallas_call(
@@ -479,12 +489,11 @@
         out_shape=jax.ShapeDtypeStruct((blocks, side, width), jnp.bfloat16),
         in_specs=[
             pl.BlockSpec(memory_space=pltpu.SMEM),
-            pl.BlockSpec(memory_space=pl.ANY),
+            pl.BlockSpec(memory_space=pltpu.VMEM),
         ],
         out_specs=pl.BlockSpec(memory_space=pl.ANY),
-        scratch_shapes=[
-            pltpu.VMEM((blocks, side, width), jnp.bfloat16), dma((groups,)), dma((groups,)),
-        ],
+        scratch_shapes=[dma((groups,))],
+        compiler_params=pltpu.CompilerParams(vmem_limit_bytes=4 * 2**20),
     )(group_order[0], hidden)
     return placed.reshape(1, rows, width)
 

time: 130 us -> 127 us (0.977)
  Pallas kernels: 130 us -> 127 us
    pallas_call x1, Pallas kernels: 127 us -> 125 us  [on_device(): pl.pallas_call(functools.partial(pipeline_kernel, sections, parts, groups...]
where the time goes in v2:
time: 127 us
  Pallas kernels  127 us (100%)
    pallas_call x1, Pallas kernels, on_device(): pl.pallas_call(functools.partial(pipeline_kernel, sections, parts, groups...  125 us

profile of v2, /device:TPU:27, one launch (start us, length us, event | category | flops | bytes accessed | tf_op | source)
XLA Modules:
  0.0 127.3 jit_solution(9811907710250195506)
XLA Ops:
  0.0 0.0 copy-start
  0.0 125.3 %shard_map.55.h_ref = bf16[16,128,512]{2,1,0:T(8,128)(2,1)S(1)} custom-call(s32[8,16]{1,0:T(8,128)} %bitcast.8, s32[1,4]{1,0:T(1,128)} %order_hbm.1, bf16[16,128,512]{2,1,0:T(8,128)(2,1)} %bitcast.6, bf16[16,8,128,128]{3,2,1,0:T(8,128)(2,1)} %adj_hbm.1, bf16[512,512]{1,0:T(8,128)(2,1)} %bitcast.7), custom_call_target="tpu_custom_call" | custom-call | tf_op jit(solution)/shard_map/pallas_call | solution.py:439
  125.4 0.0 copy-done
  125.4 1.9 %shard_map.56 = bf16[16,128,512]{2,1,0:T(8,128)(2,1)} custom-call(s32[4]{0:T(128)S(1)} %bitcast.5, bf16[16,128,512]{2,1,0:T(8,128)(2,1)S(1)} %shard_map.55.h_ref), custom_call_target="tpu_custom_call" | custom-call | tf_op jit(solution)/shard_map/pallas_call | solution.py:487
Async XLA Ops:
  0.0 125.4 %copy-start = (s32[1,4]{1,0:T(1,128)S(1)}, s32[1,4]{1,0:T(1,128)}, u32[]{:S(2)}) copy-start(s32[1,4]{1,0:T(1,128)} %order_hbm.1) | copy-start | bytes 52

commit v3 on v2

--- a/solution.py
+++ b/solution.py
@@ -10,10 +10,11 @@
 MESH = pl.DeviceIdType.MESH
 SPLIT = 2
 AHEAD = 2
+RUN = 2
 
 
 def relay_counts(blocks):
-    return blocks * 7 // 16, blocks // 8
+    return blocks * 7 // 16, 3
 
 
 def pipeline_kernel(
@@ -21,7 +22,7 @@
     columns, own_order, order_ref, x_ref, w_ref, in_sem, table, position, order_land, near_order, order_send, order_recv, order_local,
     adj, src, mine, own_land, side_land, first_land, stored_land,
     adj_sem, partner_send, partner_recv, across_send, across_recv, z_send, z_recv, f_send, f_recv,
-    over_send, over_recv, down_send, down_recv, sover_send, sover_recv, sdown_send, sdown_recv,
+    turn, over_send, over_recv, down_send, down_recv, sover_send, sover_recv, sdown_send, sdown_recv,
 ):
     s = lax.axis_index("section")
     d = lax.axis_index("dom")
@@ -54,14 +55,6 @@
     for load in loads:
         load.start()
     load_adj.start()
-    loads[0].wait()
-    loads[1].wait()
-
-    for k in range(groups):
-        piece = x_ref[pl.ds(own_order[0, k] * bg, bg)]
-        mine[k * bg:(k + 1) * bg] = piece
-        src[blocks + k * bg:blocks + (k + 1) * bg] = piece
-
     barrier = pltpu.get_barrier_semaphore()
 
     def greet(there):
@@ -86,6 +79,14 @@
         def _():
             greet(there)
 
+    loads[0].wait()
+    loads[1].wait()
+
+    for k in range(groups):
+        piece = x_ref[pl.ds(own_order[0, k] * bg, bg)]
+        mine[k * bg:(k + 1) * bg] = piece
+        src[blocks + k * bg:blocks + (k + 1) * bg] = piece
+
     pl.semaphore_wait(barrier, peers)
 
     def order_copy(way):
@@ -118,22 +119,22 @@
             device_id_type=MESH,
         )
 
-    def over_copy(b):
-        return pltpu.make_async_remote_copy(
-            src_ref=mine.at[direct + b],
-            dst_ref=first_land.at[b],
-            send_sem=over_send.at[b],
-            recv_sem=over_recv.at[b],
+    def over_copy(b, h):
+        return pltpu.make_async_remote_copy(
+            src_ref=mine.at[direct + b, pl.ds(h * half, half)],
+            dst_ref=first_land.at[b, pl.ds(h * half, half)],
+            send_sem=over_send.at[b * SPLIT + h],
+            recv_sem=over_recv.at[b * SPLIT + h],
             device_id={"section": last, "dom": across},
             device_id_type=MESH,
         )
 
-    def down_copy(b):
-        return pltpu.make_async_remote_copy(
-            src_ref=first_land.at[b],
-            dst_ref=src.at[from_across + direct + b],
-            send_sem=down_send.at[b],
-            recv_sem=down_recv.at[b],
+    def down_copy(b, h):
+        return pltpu.make_async_remote_copy(
+            src_ref=first_land.at[b, pl.ds(h * half, half)],
+            dst_ref=src.at[from_across + direct + b, pl.ds(h * half, half)],
+            send_sem=down_send.at[b * SPLIT + h],
+            recv_sem=down_recv.at[b * SPLIT + h],
             device_id={"section": 0},
             device_id_type=MESH,
         )
@@ -201,21 +202,39 @@
     for way in range(2):
         order_copy(way).start()
 
-    @pl.when(s == 0)
-    def _():
+    def hand_over(n):
+        pl.semaphore_signal(turn.at[n], inc=1, device_id={"dom": partner}, device_id_type=MESH)
+
+    def each_relay(step):
         @pl.loop(0, relayed)
         def _(b):
-            over_copy(b).start()
-
+            for h in range(SPLIT):
+                step(b, h)
+
+    @pl.when((s == 0) & (odd == 0))
+    def _():
+        each_relay(lambda b, h: over_copy(b, h).start())
         across_copy(0, 0, direct).start()
+
+    @pl.when(s == 0)
+    def _():
         partner_copy(0, blocks).start()
 
     @pl.when(s == last)
     def _():
-        @pl.loop(0, relayed)
-        def _(b):
-            over_copy(b).wait_recv()
-            down_copy(b).start()
+        def pass_down(b, h):
+            over_copy(b, h).wait_recv()
+            down_copy(b, h).start()
+
+        each_relay(pass_down)
+
+    @pl.when((s == last) & (odd == 0))
+    def _():
+        hand_over(0)
+
+    @pl.when((s == last) & (odd == 1))
+    def _():
+        pl.semaphore_wait(turn.at[0], 1)
 
     @pl.when(s == low)
     def _():
@@ -266,6 +285,20 @@
     loads[4].wait()
     own_base = jnp.where(s > 0, fresh + blocks, blocks)
 
+    @pl.when((s == 0) & (odd == 0))
+    def _():
+        each_relay(lambda b, h: over_copy(b, h).wait_send())
+        hand_over(0)
+        across_copy(0, 0, direct).wait_send()
+        hand_over(1)
+
+    @pl.when((s == 0) & (odd == 1))
+    def _():
+        pl.semaphore_wait(turn.at[0], 1)
+        each_relay(lambda b, h: over_copy(b, h).start())
+        pl.semaphore_wait(turn.at[1], 1)
+        across_copy(0, 0, direct).start()
+
     @pl.when(s == low)
     def _():
         for n, first, count in stale_pieces(stored)[:2]:
@@ -312,9 +345,7 @@
                 partner_copy(0, blocks).wait_recv()
                 across_copy(0, 0, direct).wait_recv()
 
-                @pl.loop(0, relayed)
-                def _(b):
-                    down_copy(b).wait_recv()
+                each_relay(lambda b, h: down_copy(b, h).wait_recv())
 
             @pl.when(s > 0)
             def _():
@@ -335,6 +366,11 @@
 
         @pl.loop(lo, hi)
         def _(r):
+            if k == 1:
+                @pl.when((s == 0) & (odd == 1) & (r == bg + RUN))
+                def _():
+                    pl.semaphore_wait(turn.at[2], 1)
+
             row = own_order[0, k] * bg + (r - lo)
             a = jnp.concatenate([adj[row, t] for t in range(tiles)], axis=1)
             h = jnp.concatenate([src[table[r * tiles + t]] for t in range(tiles)], axis=0)
@@ -345,14 +381,24 @@
 
             @pl.when(s < last)
             def _():
-                for h_ in range(SPLIT):
-                    up_copy(r, h_).start()
+                for n in range(SPLIT):
+                    up_copy(r, n).start()
 
             if k + 1 < groups:
                 @pl.when(s > 0)
                 def _():
                     forward(phi + AHEAD + (r - lo))
 
+        if k == 0:
+            @pl.when((s == 0) & (odd == 0))
+            def _():
+                @pl.loop(0, bg - 1)
+                def _(r):
+                    for h in range(SPLIT):
+                        up_copy(r, h).wait_send()
+
+                hand_over(2)
+
         if k + 1 < groups:
             more = per_group + (AHEAD if k + 2 < groups else 0)
 
@@ -365,17 +411,15 @@
     @pl.when(s == 0)
     def _():
         partner_copy(0, blocks).wait_send()
+
+    @pl.when((s == 0) & (odd == 1))
+    def _():
         across_copy(0, 0, direct).wait_send()
-
-        @pl.loop(0, relayed)
-        def _(b):
-            over_copy(b).wait_send()
+        each_relay(lambda b, h: over_copy(b, h).wait_send())
 
     @pl.when(s == last)
     def _():
-        @pl.loop(0, relayed)
-        def _(b):
-            down_copy(b).wait_send()
+        each_relay(lambda b, h: down_copy(b, h).wait_send())
 
     @pl.when(s == low)
     def _():
@@ -406,12 +450,14 @@
             side_copy(0, q).wait_send()
             side_copy(1, q).wait_send()
 
+    waited = jnp.where((s == 0) & (odd == 0), bg - 1, 0)
+
     @pl.when(s < last)
     def _():
-        @pl.loop(0, blocks)
+        @pl.loop(waited, blocks)
         def _(r):
-            for h_ in range(SPLIT):
-                up_copy(r, h_).wait_send()
+            for h in range(SPLIT):
+                up_copy(r, h).wait_send()
 
 
 def place_kernel(groups, order, h_ref, out_hbm, out_sem):
@@ -473,7 +519,7 @@
             dma((pieces,)),
             dma((2, pieces)),
             dma((2, pieces)),
-        ] + [dma((relayed,))] * 4 + [dma((stored,))] * 4,
+        ] + [pltpu.SemaphoreType.REGULAR((3,))] + [dma((relayed * SPLIT,))] * 4 + [dma((stored,))] * 4,
         compiler_params=pltpu.CompilerParams(
             collective_id=0, has_side_effects=True, vmem_limit_bytes=50 * 2**20
         ),

time: 127 us -> 120 us (0.945)
  Pallas kernels: 127 us -> 119 us
    pallas_call x1, Pallas kernels: 125 us -> 117 us  [on_device(): pl.pallas_call(functools.partial(pipeline_kernel, sections, parts, groups...]
where the time goes in v3:
time: 120 us; the launch traced here: 119 us
  Pallas kernels  119 us (99%)
    pallas_call x1, Pallas kernels, on_device(): pl.pallas_call(functools.partial(pipeline_kernel, sections, parts, groups...  117 us

profile of v3, /device:TPU:27, one launch (start us, length us, event | category | flops | bytes accessed | tf_op | source)
XLA Modules:
  0.0 119.1 jit_solution(7752827822624912742)
XLA Ops:
  0.0 0.0 copy-start
  0.0 117.2 %shard_map.55.h_ref = bf16[16,128,512]{2,1,0:T(8,128)(2,1)S(1)} custom-call(s32[8,16]{1,0:T(8,128)} %bitcast.8, s32[1,4]{1,0:T(1,128)} %order_hbm.1, bf16[16,128,512]{2,1,0:T(8,128)(2,1)} %bitcast.6, bf16[16,8,128,128]{3,2,1,0:T(8,128)(2,1)} %adj_hbm.1, bf16[512,512]{1,0:T(8,128)(2,1)} %bitcast.7), custom_call_target="tpu_custom_call" | custom-call | tf_op jit(solution)/shard_map/pallas_call | solution.py:485
  117.2 0.0 copy-done
  117.3 1.9 %shard_map.56 = bf16[16,128,512]{2,1,0:T(8,128)(2,1)} custom-call(s32[4]{0:T(128)S(1)} %bitcast.5, bf16[16,128,512]{2,1,0:T(8,128)(2,1)S(1)} %shard_map.55.h_ref), custom_call_target="tpu_custom_call" | custom-call | tf_op jit(solution)/shard_map/pallas_call | solution.py:533
Async XLA Ops:
  0.0 117.3 %copy-start = (s32[1,4]{1,0:T(1,128)S(1)}, s32[1,4]{1,0:T(1,128)}, u32[]{:S(2)}) copy-start(s32[1,4]{1,0:T(1,128)} %order_hbm.1) | copy-start | bytes 52

commit v4 on v3

v4 whole, which is shorter than its diff:
```python
import functools

import jax
import jax.numpy as jnp
from jax import lax
from jax.experimental import pallas as pl
from jax.experimental.pallas import tpu as pltpu
from jax.sharding import PartitionSpec as P

MESH = pl.DeviceIdType.MESH
SPLIT = 2
AHEAD = 2
FIRST_AHEAD = 0
RUN = 2
LAG = 4


def relay_counts(blocks):
    return blocks * 7 // 16, blocks * 5 // 8, blocks // 2


def pipeline_kernel(
    sections, parts, groups, columns_hbm, order_hbm, x_hbm, adj_hbm, w_hbm, out_ref,
    columns, own_order, order_ref, x_ref, w_ref, in_sem, table, position, order_land, near_order, order_send, order_recv, order_local,
    adj, src, mine, own_land, side_land, relay_in, relay_out, stored_in, stored_out,
    adj_sem, partner_send, partner_recv, across_send, across_recv, z_send, z_recv, f_send, f_recv,
    turn, lift_send, lift_recv, cross_send, cross_recv, down_send, down_recv,
    slift_send, slift_recv, scross_send, scross_recv, sdown_send, sdown_recv,
):
    s = lax.axis_index("section")
    d = lax.axis_index("dom")
    right, left = lax.rem(d + 1, parts), lax.rem(d + parts - 1, parts)
    blocks, side, width = x_ref.shape
    tiles = adj.shape[1]
    bg = blocks // groups
    fresh = 3 * blocks
    last = sections - 1
    odd = lax.rem(d, 2)
    partner = jnp.where(odd == 1, left, right)
    across = jnp.where(odd == 1, right, left)
    to_partner = jnp.where(odd == 1, 2 * blocks, 0)
    to_across = jnp.where(odd == 1, 0, 2 * blocks)
    from_across = jnp.where(odd == 1, 2 * blocks, 0)
    relayed, stored_low, stored_high = relay_counts(blocks)
    direct = blocks - relayed
    low = 1
    middle = (s > 0) & (s < last)
    stored = jnp.where(s == low, stored_low, stored_high)
    passed = jnp.where(s == low + 1, stored_low, stored_high)
    half = side // SPLIT
    aheads = [jnp.where((s == 1) & (odd == 0), FIRST_AHEAD, AHEAD)] + [AHEAD] * (groups - 2) + [0]
    per_group = bg * SPLIT

    load_adj = pltpu.make_async_copy(adj_hbm, adj, adj_sem)
    loads = [
        pltpu.make_async_copy(there, here, in_sem.at[n])
        for n, (there, here) in enumerate((
            (order_hbm, own_order), (x_hbm, x_ref), (order_hbm, order_ref),
            (columns_hbm, columns), (w_hbm, w_ref),
        ))
    ]
    for n in (2, 1, 0, 3, 4):
        loads[n].start()
    load_adj.start()
    barrier = pltpu.get_barrier_semaphore()

    def greet(there):
        pl.semaphore_signal(barrier, inc=1, device_id=there, device_id_type=MESH)

    peers = 2
    for neighbour in (left, right):
        greet({"dom": neighbour})
    for mask, there in (
        (s > 0, {"section": jnp.maximum(s - 1, 0)}),
        (s < last, {"section": jnp.minimum(s + 1, last)}),
    ):
        peers = peers + jnp.where(mask, 1, 0)

        @pl.when(mask)
        def _():
            greet(there)

    pl.semaphore_wait(barrier, peers)

    def order_copy(way):
        return pltpu.make_async_remote_copy(
            src_ref=order_ref,
            dst_ref=order_land.at[way],
            send_sem=order_send.at[way],
            recv_sem=order_recv.at[way],
            device_id={"dom": right if way == 0 else left},
            device_id_type=MESH,
        )

    def partner_copy(first, count, held=mine):
        return pltpu.make_async_remote_copy(
            src_ref=held.at[pl.ds(first, count)],
            dst_ref=src.at[pl.ds(to_partner + first, count)],
            send_sem=partner_send,
            recv_sem=partner_recv,
            device_id={"dom": partner},
            device_id_type=MESH,
        )

    def across_copy(n, first, count, held=mine):
        return pltpu.make_async_remote_copy(
            src_ref=held.at[pl.ds(first, count)],
            dst_ref=src.at[pl.ds(to_across + first, count)],
            send_sem=across_send.at[n],
            recv_sem=across_recv.at[n],
            device_id={"dom": across},
            device_id_type=MESH,
        )

    def relay_copy(held, landing, send, recv, there):
        return pltpu.make_async_remote_copy(
            src_ref=held, dst_ref=landing, send_sem=send, recv_sem=recv,
            device_id=there, device_id_type=MESH,
        )

    def lift(b, h):
        part, q = pl.ds(h * half, half), b * SPLIT + h
        return relay_copy(
            x_ref.at[direct + b, part], relay_in.at[b, part],
            lift_send.at[q], lift_recv.at[q], {"section": low},
        )

    def cross(b, h):
        part, q = pl.ds(h * half, half), b * SPLIT + h
        return relay_copy(
            relay_in.at[b, part], relay_out.at[b, part],
            cross_send.at[q], cross_recv.at[q], {"dom": across},
        )

    def down(b, h):
        part, q = pl.ds(h * half, half), b * SPLIT + h
        return relay_copy(
            relay_out.at[b, part], src.at[from_across + direct + b, part],
            down_send.at[q], down_recv.at[q], {"section": 0},
        )

    def stored_lift(b, count):
        return relay_copy(
            mine.at[blocks - count + b], stored_in.at[b],
            slift_send.at[b], slift_recv.at[b], {"section": jnp.minimum(s + 1, last)},
        )

    def stored_cross(b):
        return relay_copy(
            stored_in.at[b], stored_out.at[b],
            scross_send.at[b], scross_recv.at[b], {"dom": across},
        )

    def stored_down(b, count):
        return relay_copy(
            stored_out.at[b], src.at[from_across + blocks - count + b],
            sdown_send.at[b], sdown_recv.at[b], {"section": jnp.maximum(s - 1, 0)},
        )

    def up_copy(r, h):
        q = r * SPLIT + h
        return pltpu.make_async_remote_copy(
            src_ref=out_ref.at[r, pl.ds(h * half, half)],
            dst_ref=own_land.at[q],
            send_sem=z_send.at[q],
            recv_sem=z_recv.at[q],
            device_id={"section": jnp.minimum(s + 1, last)},
            device_id_type=MESH,
        )

    def up_wait(q):
        pltpu.make_async_remote_copy(
            src_ref=own_land.at[q],
            dst_ref=own_land.at[q],
            send_sem=z_send.at[q],
            recv_sem=z_recv.at[q],
            device_id={"section": jnp.minimum(s + 1, last)},
            device_id_type=MESH,
        ).wait_recv()

    def side_copy(way, q):
        return pltpu.make_async_remote_copy(
            src_ref=own_land.at[q],
            dst_ref=side_land.at[way, q],
            send_sem=f_send.at[way, q],
            recv_sem=f_recv.at[way, q],
            device_id={"dom": right if way == 0 else left},
            device_id_type=MESH,
        )

    def forward(q):
        up_wait(q)
        side_copy(0, q).start()
        side_copy(1, q).start()

    def stale_across(kept):
        return across_copy(0, bg, blocks - bg - kept)

    loads[2].wait()
    for way in range(2):
        order_copy(way).start()

    loads[1].wait()

    def hand_over(n):
        pl.semaphore_signal(turn.at[n], inc=1, device_id={"dom": partner}, device_id_type=MESH)

    def each_relay(step):
        @pl.loop(0, relayed)
        def _(b):
            for h in range(SPLIT):
                step(b, h)

    @pl.when((s == 0) & (odd == 0))
    def _():
        each_relay(lambda b, h: lift(b, h).start())
        across_copy(0, 0, direct, x_ref).start()

    @pl.when(s == 0)
    def _():
        partner_copy(0, blocks, x_ref).start()
        src[blocks:2 * blocks] = x_ref[...]

    loads[0].wait()

    @pl.when(s > 0)
    def _():
        for k in range(groups):
            piece = x_ref[pl.ds(own_order[0, k] * bg, bg)]
            mine[k * bg:(k + 1) * bg] = piece
            src[blocks + k * bg:blocks + (k + 1) * bg] = piece


    @pl.when(s > 0)
    def _():
        partner_copy(bg, blocks - bg).start()

    @pl.when(middle)
    def _():
        @pl.loop(0, stored)
        def _(b):
            stored_lift(b, stored).start()

    def pass_across(b, h):
        lift(b, h).wait_recv()
        cross(b, h).start()

    def pass_down(b, h):
        cross(b, h).wait_recv()
        down(b, h).start()

    @pl.when((s == low) & (odd == 0))
    def _():
        each_relay(pass_across)
        each_relay(pass_down)

    @pl.when((s == low) & (odd == 1))
    def _():
        @pl.loop(0, relayed - LAG // SPLIT)
        def _(b):
            for h in range(SPLIT):
                pass_down(b, h)

        @pl.loop(0, LAG // SPLIT)
        def _(b):
            for h in range(SPLIT):
                pass_across(b, h)
                pass_down(relayed - LAG // SPLIT + b, h)

        @pl.loop(LAG // SPLIT, relayed)
        def _(b):
            for h in range(SPLIT):
                pass_across(b, h)

    @pl.when(s == low)
    def _():
        stale_across(stored_low).start()

    @pl.when(s > low)
    def _():
        def stored_pass_across(b):
            stored_lift(b, passed).wait_recv()
            stored_cross(b).start()

        def stored_pass_down(b):
            stored_cross(b).wait_recv()
            stored_down(b, passed).start()

        stored_pass_across(0)
        stored_pass_across(1)

        @pl.loop(2, passed)
        def _(b):
            stored_pass_across(b)
            stored_pass_down(b - 2)

        @pl.when(s == last)
        def _():
            stale_across(0).start()

        @pl.when(s < last)
        def _():
            stale_across(stored_high).start()

        stored_pass_down(passed - 2)
        stored_pass_down(passed - 1)

    for way in range(2):
        order_copy(way).wait()
        local = pltpu.make_async_copy(
            order_land.at[way], near_order.at[way], order_local.at[way]
        )
        local.start()
        local.wait()

    for p in range(3):
        for g in range(groups):
            step = jnp.int32(0)
            for k in range(1, groups):
                held = own_order[0, k] if p == 1 else near_order[p // 2, 0, k]
                step = jnp.where(held == g, k, step)
            position[p * groups + g] = step

    later = s > 0
    loads[3].wait()

    @pl.loop(0, blocks)
    def _(r):
        k = r // bg
        row = own_order[0, k] * bg + r % bg
        for t in range(tiles):
            column = columns[t, row]
            relative = jnp.minimum(lax.rem(lax.div(column, blocks) - d + 1 + parts, parts), 2)
            inside = lax.rem(column, blocks)
            step = position[relative * groups + lax.div(inside, bg)]
            place = jnp.where(later, step * bg + lax.rem(inside, bg), inside)
            slot = relative * blocks + place
            table[r * tiles + t] = slot + jnp.where(later & (step <= k), fresh, 0)

    load_adj.wait()
    loads[4].wait()

    @pl.when((s == 0) & (odd == 0))
    def _():
        each_relay(lambda b, h: lift(b, h).wait_send())
        hand_over(0)
        across_copy(0, 0, direct, x_ref).wait_send()
        hand_over(1)

    @pl.when((s == 0) & (odd == 1))
    def _():
        pl.semaphore_wait(turn.at[0], 1)
        each_relay(lambda b, h: lift(b, h).start())
        pl.semaphore_wait(turn.at[1], 1)
        across_copy(0, 0, direct, x_ref).start()

    for k in range(groups):
        lo, hi = k * bg, (k + 1) * bg
        plo, phi = lo * SPLIT, hi * SPLIT

        @pl.when(s > 0)
        def _():
            if k == 0:
                @pl.loop(0, per_group + aheads[0])
                def _(q):
                    forward(q)

            def as_blocks(pieces):
                return pieces.reshape(bg, side, width)

            src[fresh + blocks + lo:fresh + blocks + hi] = as_blocks(own_land[plo:phi])

            @pl.loop(lo, hi)
            def _(r):
                for way in range(2):
                    for n in range(SPLIT):
                        side_copy(way, r * SPLIT + n).wait_recv()
                    block = side_land[way, pl.ds(r * SPLIT, SPLIT)]
                    src[fresh + 2 * way * blocks + r] = block.reshape(side, width)

        if k == 0:
            @pl.when(s == 0)
            def _():
                partner_copy(0, blocks, x_ref).wait_recv()
                across_copy(0, 0, direct, x_ref).wait_recv()

                each_relay(lambda b, h: down(b, h).wait_recv())

            @pl.when(s > 0)
            def _():
                partner_copy(bg, blocks - bg).wait_recv()

            @pl.when(middle)
            def _():
                @pl.when(s == low)
                def _():
                    stale_across(stored_low).wait_recv()

                @pl.when(s > low)
                def _():
                    stale_across(stored_high).wait_recv()

                @pl.loop(0, stored)
                def _(b):
                    stored_down(b, stored).wait_recv()

            @pl.when(s == last)
            def _():
                stale_across(0).wait_recv()

        def layer_row(r):
            row = own_order[0, k] * bg + (r - lo)
            a = jnp.concatenate([adj[row, t] for t in range(tiles)], axis=1)
            h = jnp.concatenate([src[table[r * tiles + t]] for t in range(tiles)], axis=0)
            agg = jnp.dot(a, h, preferred_element_type=jnp.float32).astype(jnp.bfloat16)
            product = jnp.dot(agg, w_ref[...], preferred_element_type=jnp.float32)
            own = jnp.where(later, fresh + blocks + r, blocks + row)
            before = src[own].astype(jnp.float32)
            out_ref[r] = (before + jnp.maximum(product, 0.0)).astype(jnp.bfloat16)

        closing = (s == last) if k == groups - 1 else (s < 0)
        if k == groups - 1:
            @pl.when(closing)
            def _():
                for r in range(lo, hi):
                    layer_row(r)

        @pl.loop(lo, jnp.where(closing, lo, hi))
        def _(r):
            if k == 1:
                @pl.when((s == 0) & (odd == 1) & (r == bg + RUN))
                def _():
                    pl.semaphore_wait(turn.at[2], 1)

            layer_row(r)

            @pl.when(s < last)
            def _():
                for n in range(SPLIT):
                    up_copy(r, n).start()

            if k + 1 < groups:
                @pl.when(s > 0)
                def _():
                    forward(phi + aheads[k] + (r - lo))

        if k == 0:
            @pl.when((s == 0) & (odd == 0))
            def _():
                @pl.loop(0, bg - 1)
                def _(r):
                    for h in range(SPLIT):
                        up_copy(r, h).wait_send()

                hand_over(2)

        if k + 1 < groups:
            more = per_group + aheads[k + 1]

            @pl.when(s > 0)
            def _():
                @pl.loop(phi + aheads[k] + bg, phi + more)
                def _(q):
                    forward(q)

    @pl.when(s == 0)
    def _():
        partner_copy(0, blocks, x_ref).wait_send()

    @pl.when((s == 0) & (odd == 1))
    def _():
        across_copy(0, 0, direct, x_ref).wait_send()
        each_relay(lambda b, h: lift(b, h).wait_send())

    @pl.when(s == low)
    def _():
        each_relay(lambda b, h: cross(b, h).wait_send())
        each_relay(lambda b, h: down(b, h).wait_send())

    @pl.when(middle)
    def _():
        @pl.when(s == low)
        def _():
            stale_across(stored_low).wait_send()

        @pl.when(s > low)
        def _():
            stale_across(stored_high).wait_send()

        @pl.loop(0, stored)
        def _(b):
            stored_lift(b, stored).wait_send()

    @pl.when(s == last)
    def _():
        stale_across(0).wait_send()

    @pl.when(s > low)
    def _():
        @pl.loop(0, passed)
        def _(b):
            stored_cross(b).wait_send()
            stored_down(b, passed).wait_send()

    @pl.when(s > 0)
    def _():
        partner_copy(bg, blocks - bg).wait_send()

        @pl.loop(0, blocks * SPLIT)
        def _(q):
            side_copy(0, q).wait_send()
            side_copy(1, q).wait_send()

    waited = jnp.where((s == 0) & (odd == 0), bg - 1, 0)

    @pl.when(s < last)
    def _():
        @pl.loop(waited, blocks)
        def _(r):
            for h in range(SPLIT):
                up_copy(r, h).wait_send()


def place_kernel(groups, order, h_ref, out_hbm, out_sem):
    bg = h_ref.shape[0] // groups

    def store(k):
        return pltpu.make_async_copy(
            h_ref.at[pl.ds(k * bg, bg)], out_hbm.at[pl.ds(order[k] * bg, bg)], out_sem.at[k]
        )

    for k in range(groups):
        store(k).start()
    for k in range(groups):
        store(k).wait()


def on_device(sections, layer_inputs, adjacency, columns, group_order, weights):
    parts = lax.axis_size("dom")
    rows, width = layer_inputs.shape[1:]
    blocks, tiles, side = adjacency.shape[:3]
    groups = group_order.shape[1]
    relayed, stored, _ = relay_counts(blocks)
    pieces = blocks * SPLIT
    dma = pltpu.SemaphoreType.DMA
    hidden = pl.pallas_call(
        functools.partial(pipeline_kernel, sections, parts, groups),
        out_shape=jax.ShapeDtypeStruct((blocks, side, width), jnp.bfloat16),
        in_specs=[
            pl.BlockSpec(memory_space=pltpu.HBM) for _ in range(5)
        ],
        out_specs=pl.BlockSpec(memory_space=pltpu.VMEM),
        scratch_shapes=[
            pltpu.SMEM((tiles, blocks), jnp.int32),
            pltpu.SMEM((1, groups), jnp.int32),
            pltpu.VMEM((1, groups), jnp.int32),
            pltpu.VMEM((blocks, side, width), jnp.bfloat16),
            pltpu.VMEM((width, width), jnp.bfloat16),
            dma((5,)),
            pltpu.SMEM((blocks * tiles,), jnp.int32),
            pltpu.SMEM((3 * groups,), jnp.int32),
            pltpu.VMEM((2, 1, groups), jnp.int32),
            pltpu.SMEM((2, 1, groups), jnp.int32),
            dma((2,)),
            dma((2,)),
            dma((2,)),
            pltpu.VMEM(adjacency.shape, jnp.bfloat16),
            pltpu.VMEM((6 * blocks, side, width), jnp.bfloat16),
            pltpu.VMEM((blocks, side, width), jnp.bfloat16),
            pltpu.VMEM((pieces, side // SPLIT, width), jnp.bfloat16),
            pltpu.VMEM((2, pieces, side // SPLIT, width), jnp.bfloat16),
            pltpu.VMEM((relayed, side, width), jnp.bfloat16),
            pltpu.VMEM((relayed, side, width), jnp.bfloat16),
            pltpu.VMEM((stored, side, width), jnp.bfloat16),
            pltpu.VMEM((stored, side, width), jnp.bfloat16),
            dma,
            dma,
            dma,
            dma((1,)),
            dma((1,)),
            dma((pieces,)),
            dma((pieces,)),
            dma((2, pieces)),
            dma((2, pieces)),
        ] + [pltpu.SemaphoreType.REGULAR((3,))]
        + [dma((relayed * SPLIT,))] * 6 + [dma((stored,))] * 6,
        compiler_params=pltpu.CompilerParams(
            collective_id=0, has_side_effects=True, vmem_limit_bytes=50 * 2**20
        ),
    )(
        *(pltpu.with_memory_space_constraint(array, pltpu.HBM) for array in (
            columns.T, group_order, layer_inputs.reshape(blocks, side, width),
            adjacency, weights[0],
        ))
    )

    placed = pl.pallas_call(
        functools.partial(place_kernel, groups),
        out_shape=jax.ShapeDtypeStruct((blocks, side, width), jnp.bfloat16),
        in_specs=[
            pl.BlockSpec(memory_space=pltpu.SMEM),
            pl.BlockSpec(memory_space=pltpu.VMEM),
        ],
        out_specs=pl.BlockSpec(memory_space=pl.ANY),
        scratch_shapes=[dma((groups,))],
        compiler_params=pltpu.CompilerParams(vmem_limit_bytes=4 * 2**20),
    )(group_order[0], hidden)
    return placed.reshape(1, rows, width)


def solution(mesh):
    in_specs = (
        P("section", "dom", None),
        P("dom", None, None, None),
        P("dom", None),
        P("dom", None),
        P("section", None, None),
    )
    return jax.shard_map(
        functools.partial(on_device, mesh.shape["section"]),
        mesh=mesh, in_specs=in_specs, out_specs=P("section", "dom", None), check_vma=False,
    )
```

time: 120 us -> 119 us (level); the launches traced: 119 us -> 117 us
  Pallas kernels: 119 us -> 117 us
    pallas_call x1, Pallas kernels: 117 us -> 115 us  [on_device(): pl.pallas_call(functools.partial(pipeline_kernel, sections, parts, groups...]
where the time goes in v4:
time: 119 us; the launch traced here: 117 us
  Pallas kernels  117 us (98%)
    pallas_call x1, Pallas kernels, on_device(): pl.pallas_call(functools.partial(pipeline_kernel, sections, parts, groups...  115 us

profile of v4, /device:TPU:27, one launch (start us, length us, event | category | flops | bytes accessed | tf_op | source)
XLA Modules:
  0.0 116.9 jit_solution(3249212433063362092)
XLA Ops:
  0.0 0.0 copy-start
  0.0 115.0 %shard_map.55.h_ref = bf16[16,128,512]{2,1,0:T(8,128)(2,1)S(1)} custom-call(s32[8,16]{1,0:T(8,128)} %bitcast.8, s32[1,4]{1,0:T(1,128)} %order_hbm.1, bf16[16,128,512]{2,1,0:T(8,128)(2,1)} %bitcast.6, bf16[16,8,128,128]{3,2,1,0:T(8,128)(2,1)} %adj_hbm.1, bf16[512,512]{1,0:T(8,128)(2,1)} %bitcast.7), custom_call_target="tpu_custom_call" | custom-call | tf_op jit(solution)/shard_map/pallas_call | solution.py:546
  115.0 0.0 copy-done
  115.0 1.9 %shard_map.56 = bf16[16,128,512]{2,1,0:T(8,128)(2,1)} custom-call(s32[4]{0:T(128)S(1)} %bitcast.5, bf16[16,128,512]{2,1,0:T(8,128)(2,1)S(1)} %shard_map.55.h_ref), custom_call_target="tpu_custom_call" | custom-call | tf_op jit(solution)/shard_map/pallas_call | solution.py:597
Async XLA Ops:
  0.0 115.0 %copy-start = (s32[1,4]{1,0:T(1,128)S(1)}, s32[1,4]{1,0:T(1,128)}, u32[]{:S(2)}) copy-start(s32[1,4]{1,0:T(1,128)} %order_hbm.1) | copy-start | bytes 52

commit v5 on v4

--- a/solution.py
+++ b/solution.py
@@ -118,43 +118,76 @@
             device_id=there, device_id_type=MESH,
         )
 
+    def lifts():
+        return relay_copy(
+            x_ref.at[pl.ds(direct, relayed)], relay_in, lift_send, lift_recv.at[0],
+            {"section": low},
+        )
+
+    def crosses():
+        return relay_copy(relay_in, relay_out, cross_send, cross_recv.at[0], {"dom": across})
+
+    def downs():
+        return relay_copy(
+            relay_out, src.at[pl.ds(from_across + direct, relayed)], down_send, down_recv,
+            {"section": 0},
+        )
+
     def lift(b, h):
         part, q = pl.ds(h * half, half), b * SPLIT + h
         return relay_copy(
             x_ref.at[direct + b, part], relay_in.at[b, part],
-            lift_send.at[q], lift_recv.at[q], {"section": low},
+            lift_send, lift_recv.at[q], {"section": low},
         )
 
     def cross(b, h):
         part, q = pl.ds(h * half, half), b * SPLIT + h
         return relay_copy(
             relay_in.at[b, part], relay_out.at[b, part],
-            cross_send.at[q], cross_recv.at[q], {"dom": across},
+            cross_send, cross_recv.at[q], {"dom": across},
         )
 
     def down(b, h):
         part, q = pl.ds(h * half, half), b * SPLIT + h
         return relay_copy(
             relay_out.at[b, part], src.at[from_across + direct + b, part],
-            down_send.at[q], down_recv.at[q], {"section": 0},
+            down_send, down_recv, {"section": 0},
         )
 
     def stored_lift(b, count):
         return relay_copy(
             mine.at[blocks - count + b], stored_in.at[b],
-            slift_send.at[b], slift_recv.at[b], {"section": jnp.minimum(s + 1, last)},
+            slift_send, slift_recv.at[b], {"section": jnp.minimum(s + 1, last)},
         )
 
     def stored_cross(b):
         return relay_copy(
             stored_in.at[b], stored_out.at[b],
-            scross_send.at[b], scross_recv.at[b], {"dom": across},
+            scross_send, scross_recv.at[b], {"dom": across},
         )
 
     def stored_down(b, count):
         return relay_copy(
             stored_out.at[b], src.at[from_across + blocks - count + b],
-            sdown_send.at[b], sdown_recv.at[b], {"section": jnp.maximum(s - 1, 0)},
+            sdown_send, sdown_recv, {"section": jnp.maximum(s - 1, 0)},
+        )
+
+    def stored_lifts(count):
+        return relay_copy(
+            mine.at[pl.ds(blocks - count, count)], stored_in.at[pl.ds(0, count)],
+            slift_send, slift_recv.at[0], {"section": jnp.minimum(s + 1, last)},
+        )
+
+    def stored_crosses(count):
+        return relay_copy(
+            stored_in.at[pl.ds(0, count)], stored_out.at[pl.ds(0, count)],
+            scross_send, scross_recv.at[0], {"dom": across},
+        )
+
+    def stored_downs(count):
+        return relay_copy(
+            stored_out.at[pl.ds(0, count)], src.at[pl.ds(from_across + blocks - count, count)],
+            sdown_send, sdown_recv, {"section": jnp.maximum(s - 1, 0)},
         )
 
     def up_copy(r, h):
@@ -162,17 +195,26 @@
         return pltpu.make_async_remote_copy(
             src_ref=out_ref.at[r, pl.ds(h * half, half)],
             dst_ref=own_land.at[q],
-            send_sem=z_send.at[q],
+            send_sem=z_send.at[jnp.where(r < bg - 1, 0, 1)],
             recv_sem=z_recv.at[q],
             device_id={"section": jnp.minimum(s + 1, last)},
             device_id_type=MESH,
         )
+
+    def up_sent(n):
+        cut = (bg - 1) * SPLIT
+        part = pl.ds(0, cut) if n == 0 else pl.ds(cut, blocks * SPLIT - cut)
+        pltpu.make_async_remote_copy(
+            src_ref=own_land.at[part], dst_ref=own_land.at[part],
+            send_sem=z_send.at[n], recv_sem=z_recv.at[0],
+            device_id={"section": jnp.minimum(s + 1, last)}, device_id_type=MESH,
+        ).wait_send()
 
     def up_wait(q):
         pltpu.make_async_remote_copy(
             src_ref=own_land.at[q],
             dst_ref=own_land.at[q],
-            send_sem=z_send.at[q],
+            send_sem=z_send.at[0],
             recv_sem=z_recv.at[q],
             device_id={"section": jnp.minimum(s + 1, last)},
             device_id_type=MESH,
@@ -182,11 +224,29 @@
         return pltpu.make_async_remote_copy(
             src_ref=own_land.at[q],
             dst_ref=side_land.at[way, q],
-            send_sem=f_send.at[way, q],
-            recv_sem=f_recv.at[way, q],
+            send_sem=f_send.at[way],
+            recv_sem=f_recv.at[way, q // SPLIT],
             device_id={"dom": right if way == 0 else left},
             device_id_type=MESH,
         )
+
+    def side_block(way, r):
+        part = pl.ds(r * SPLIT, SPLIT)
+        return pltpu.make_async_remote_copy(
+            src_ref=own_land.at[part],
+            dst_ref=side_land.at[way, part],
+            send_sem=f_send.at[way],
+            recv_sem=f_recv.at[way, r],
+            device_id={"dom": right if way == 0 else left},
+            device_id_type=MESH,
+        )
+
+    def side_sent(way):
+        pltpu.make_async_remote_copy(
+            src_ref=own_land, dst_ref=side_land.at[way],
+            send_sem=f_send.at[way], recv_sem=f_recv.at[way, 0],
+            device_id={"dom": right if way == 0 else left}, device_id_type=MESH,
+        ).wait_send()
 
     def forward(q):
         up_wait(q)
@@ -342,7 +402,7 @@
 
     @pl.when((s == 0) & (odd == 0))
     def _():
-        each_relay(lambda b, h: lift(b, h).wait_send())
+        lifts().wait_send()
         hand_over(0)
         across_copy(0, 0, direct, x_ref).wait_send()
         hand_over(1)
@@ -373,8 +433,7 @@
             @pl.loop(lo, hi)
             def _(r):
                 for way in range(2):
-                    for n in range(SPLIT):
-                        side_copy(way, r * SPLIT + n).wait_recv()
+                    side_block(way, r).wait_recv()
                     block = side_land[way, pl.ds(r * SPLIT, SPLIT)]
                     src[fresh + 2 * way * blocks + r] = block.reshape(side, width)
 
@@ -384,7 +443,7 @@
                 partner_copy(0, blocks, x_ref).wait_recv()
                 across_copy(0, 0, direct, x_ref).wait_recv()
 
-                each_relay(lambda b, h: down(b, h).wait_recv())
+                downs().wait_recv()
 
             @pl.when(s > 0)
             def _():
@@ -395,14 +454,12 @@
                 @pl.when(s == low)
                 def _():
                     stale_across(stored_low).wait_recv()
+                    stored_downs(stored_low).wait_recv()
 
                 @pl.when(s > low)
                 def _():
                     stale_across(stored_high).wait_recv()
-
-                @pl.loop(0, stored)
-                def _(b):
-                    stored_down(b, stored).wait_recv()
+                    stored_downs(stored_high).wait_recv()
 
             @pl.when(s == last)
             def _():
@@ -447,11 +504,7 @@
         if k == 0:
             @pl.when((s == 0) & (odd == 0))
             def _():
-                @pl.loop(0, bg - 1)
-                def _(r):
-                    for h in range(SPLIT):
-                        up_copy(r, h).wait_send()
-
+                up_sent(0)
                 hand_over(2)
 
         if k + 1 < groups:
@@ -470,55 +523,46 @@
     @pl.when((s == 0) & (odd == 1))
     def _():
         across_copy(0, 0, direct, x_ref).wait_send()
-        each_relay(lambda b, h: lift(b, h).wait_send())
+        lifts().wait_send()
 
     @pl.when(s == low)
     def _():
-        each_relay(lambda b, h: cross(b, h).wait_send())
-        each_relay(lambda b, h: down(b, h).wait_send())
-
-    @pl.when(middle)
-    def _():
-        @pl.when(s == low)
+        crosses().wait_send()
+        downs().wait_send()
+
+    @pl.when(s == low)
+    def _():
+        stale_across(stored_low).wait_send()
+        stored_lifts(stored_low).wait_send()
+
+    @pl.when((s > low) & (s < last))
+    def _():
+        stale_across(stored_high).wait_send()
+        stored_lifts(stored_high).wait_send()
+
+    @pl.when(s == last)
+    def _():
+        stale_across(0).wait_send()
+
+    for mask, count in ((s == low + 1, stored_low), (s > low + 1, stored_high)):
+        @pl.when(mask)
         def _():
-            stale_across(stored_low).wait_send()
-
-        @pl.when(s > low)
-        def _():
-            stale_across(stored_high).wait_send()
-
-        @pl.loop(0, stored)
-        def _(b):
-            stored_lift(b, stored).wait_send()
-
-    @pl.when(s == last)
-    def _():
-        stale_across(0).wait_send()
-
-    @pl.when(s > low)
-    def _():
-        @pl.loop(0, passed)
-        def _(b):
-            stored_cross(b).wait_send()
-            stored_down(b, passed).wait_send()
+            stored_crosses(count).wait_send()
+            stored_downs(count).wait_send()
 
     @pl.when(s > 0)
     def _():
         partner_copy(bg, blocks - bg).wait_send()
-
-        @pl.loop(0, blocks * SPLIT)
-        def _(q):
-            side_copy(0, q).wait_send()
-            side_copy(1, q).wait_send()
-
-    waited = jnp.where((s == 0) & (odd == 0), bg - 1, 0)
+        for way in range(2):
+            side_sent(way)
+
+    @pl.when((s < last) & ((s > 0) | (odd == 1)))
+    def _():
+        up_sent(0)
 
     @pl.when(s < last)
     def _():
-        @pl.loop(waited, blocks)
-        def _(r):
-            for h in range(SPLIT):
-                up_copy(r, h).wait_send()
+        up_sent(1)
 
 
 def place_kernel(groups, order, h_ref, out_hbm, out_sem):
@@ -578,12 +622,12 @@
             dma,
             dma((1,)),
             dma((1,)),
+            dma((2,)),
             dma((pieces,)),
-            dma((pieces,)),
-            dma((2, pieces)),
-            dma((2, pieces)),
+            dma((2,)),
+            dma((2, blocks)),
         ] + [pltpu.SemaphoreType.REGULAR((3,))]
-        + [dma((relayed * SPLIT,))] * 6 + [dma((stored,))] * 6,
+        + [dma, dma((relayed * SPLIT,))] * 2 + [dma, dma] + [dma, dma((stored,))] * 2 + [dma, dma],
         compiler_params=pltpu.CompilerParams(
             collective_id=0, has_side_effects=True, vmem_limit_bytes=50 * 2**20
         ),

time: 119 us -> 117 us (0.983)
  Pallas kernels: 117 us -> 115 us
    pallas_call x1, Pallas kernels: 115 us -> 113 us  [on_device(): pl.pallas_call(functools.partial(pipeline_kernel, sections, parts, groups...]
where the time goes in v5:
time: 117 us; the launch traced here: 115 us
  Pallas kernels  115 us (98%)
    pallas_call x1, Pallas kernels, on_device(): pl.pallas_call(functools.partial(pipeline_kernel, sections, parts, groups...  113 us

profile of v5, /device:TPU:27, one launch (start us, length us, event | category | flops | bytes accessed | tf_op | source)
XLA Modules:
  0.0 115.2 jit_solution(843025154670699142)
XLA Ops:
  0.0 0.0 copy-start
  0.0 113.2 %shard_map.55.h_ref = bf16[16,128,512]{2,1,0:T(8,128)(2,1)S(1)} custom-call(s32[8,16]{1,0:T(8,128)} %bitcast.8, s32[1,4]{1,0:T(1,128)} %order_hbm.1, bf16[16,128,512]{2,1,0:T(8,128)(2,1)} %bitcast.6, bf16[16,8,128,128]{3,2,1,0:T(8,128)(2,1)} %adj_hbm.1, bf16[512,512]{1,0:T(8,128)(2,1)} %bitcast.7), custom_call_target="tpu_custom_call" | custom-call | tf_op jit(solution)/shard_map/pallas_call | solution.py:590
  113.3 0.0 copy-done
  113.3 1.9 %shard_map.56 = bf16[16,128,512]{2,1,0:T(8,128)(2,1)} custom-call(s32[4]{0:T(128)S(1)} %bitcast.5, bf16[16,128,512]{2,1,0:T(8,128)(2,1)S(1)} %shard_map.55.h_ref), custom_call_target="tpu_custom_call" | custom-call | tf_op jit(solution)/shard_map/pallas_call | solution.py:641
Async XLA Ops:
  0.0 113.3 %copy-start = (s32[1,4]{1,0:T(1,128)S(1)}, s32[1,4]{1,0:T(1,128)}, u32[]{:S(2)}) copy-start(s32[1,4]{1,0:T(1,128)} %order_hbm.1) | copy-start | bytes 52

commit v6 on v5

--- a/solution.py
+++ b/solution.py
@@ -9,7 +9,8 @@
 
 MESH = pl.DeviceIdType.MESH
 SPLIT = 2
-AHEAD = 2
+UP = 4
+AHEAD = 4
 FIRST_AHEAD = 0
 RUN = 2
 LAG = 4
@@ -49,7 +50,9 @@
     passed = jnp.where(s == low + 1, stored_low, stored_high)
     half = side // SPLIT
     aheads = [jnp.where((s == 1) & (odd == 0), FIRST_AHEAD, AHEAD)] + [AHEAD] * (groups - 2) + [0]
-    per_group = bg * SPLIT
+    per_group = bg * UP
+    short = side // UP
+    a_row = UP // 2
 
     load_adj = pltpu.make_async_copy(adj_hbm, adj, adj_sem)
     loads = [
@@ -191,9 +194,9 @@
         )
 
     def up_copy(r, h):
-        q = r * SPLIT + h
+        q = r * UP + h
         return pltpu.make_async_remote_copy(
-            src_ref=out_ref.at[r, pl.ds(h * half, half)],
+            src_ref=out_ref.at[r, pl.ds(h * short, short)],
             dst_ref=own_land.at[q],
             send_sem=z_send.at[jnp.where(r < bg - 1, 0, 1)],
             recv_sem=z_recv.at[q],
@@ -202,8 +205,8 @@
         )
 
     def up_sent(n):
-        cut = (bg - 1) * SPLIT
-        part = pl.ds(0, cut) if n == 0 else pl.ds(cut, blocks * SPLIT - cut)
+        cut = (bg - 1) * UP
+        part = pl.ds(0, cut) if n == 0 else pl.ds(cut, blocks * UP - cut)
         pltpu.make_async_remote_copy(
             src_ref=own_land.at[part], dst_ref=own_land.at[part],
             send_sem=z_send.at[n], recv_sem=z_recv.at[0],
@@ -225,13 +228,13 @@
             src_ref=own_land.at[q],
             dst_ref=side_land.at[way, q],
             send_sem=f_send.at[way],
-            recv_sem=f_recv.at[way, q // SPLIT],
+            recv_sem=f_recv.at[way, q // UP],
             device_id={"dom": right if way == 0 else left},
             device_id_type=MESH,
         )
 
     def side_block(way, r):
-        part = pl.ds(r * SPLIT, SPLIT)
+        part = pl.ds(r * UP, UP)
         return pltpu.make_async_remote_copy(
             src_ref=own_land.at[part],
             dst_ref=side_land.at[way, part],
@@ -416,7 +419,7 @@
 
     for k in range(groups):
         lo, hi = k * bg, (k + 1) * bg
-        plo, phi = lo * SPLIT, hi * SPLIT
+        plo, phi = lo * UP, hi * UP
 
         @pl.when(s > 0)
         def _():
@@ -434,7 +437,7 @@
             def _(r):
                 for way in range(2):
                     side_block(way, r).wait_recv()
-                    block = side_land[way, pl.ds(r * SPLIT, SPLIT)]
+                    block = side_land[way, pl.ds(r * UP, UP)]
                     src[fresh + 2 * way * blocks + r] = block.reshape(side, width)
 
         if k == 0:
@@ -493,13 +496,14 @@
 
             @pl.when(s < last)
             def _():
-                for n in range(SPLIT):
+                for n in range(UP):
                     up_copy(r, n).start()
 
             if k + 1 < groups:
                 @pl.when(s > 0)
                 def _():
-                    forward(phi + aheads[k] + (r - lo))
+                    for n in range(a_row):
+                        forward(phi + aheads[k] + (r - lo) * a_row + n)
 
         if k == 0:
             @pl.when((s == 0) & (odd == 0))
@@ -512,7 +516,7 @@
 
             @pl.when(s > 0)
             def _():
-                @pl.loop(phi + aheads[k] + bg, phi + more)
+                @pl.loop(phi + aheads[k] + bg * a_row, phi + more)
                 def _(q):
                     forward(q)
 
@@ -585,7 +589,7 @@
     blocks, tiles, side = adjacency.shape[:3]
     groups = group_order.shape[1]
     relayed, stored, _ = relay_counts(blocks)
-    pieces = blocks * SPLIT
+    pieces = blocks * UP
     dma = pltpu.SemaphoreType.DMA
     hidden = pl.pallas_call(
         functools.partial(pipeline_kernel, sections, parts, groups),
@@ -611,8 +615,8 @@
             pltpu.VMEM(adjacency.shape, jnp.bfloat16),
             pltpu.VMEM((6 * blocks, side, width), jnp.bfloat16),
             pltpu.VMEM((blocks, side, width), jnp.bfloat16),
-            pltpu.VMEM((pieces, side // SPLIT, width), jnp.bfloat16),
-            pltpu.VMEM((2, pieces, side // SPLIT, width), jnp.bfloat16),
+            pltpu.VMEM((pieces, side // UP, width), jnp.bfloat16),
+            pltpu.VMEM((2, pieces, side // UP, width), jnp.bfloat16),
             pltpu.VMEM((relayed, side, width), jnp.bfloat16),
             pltpu.VMEM((relayed, side, width), jnp.bfloat16),
             pltpu.VMEM((stored, side, width), jnp.bfloat16),

time: 117 us -> 116 us (level)
  no operation moved by 1% of the time
where the time goes in v6:
time: 116 us; the launch traced here: 115 us
  Pallas kernels  115 us (99%)
    pallas_call x1, Pallas kernels, on_device(): pl.pallas_call(functools.partial(pipeline_kernel, sections, parts, groups...  113 us

profile of v6, /device:TPU:27, one launch (start us, length us, event | category | flops | bytes accessed | tf_op | source)
XLA Modules:
  0.0 115.0 jit_solution(13620279638460965414)
XLA Ops:
  0.0 0.0 copy-start
  0.0 113.1 %shard_map.55.h_ref = bf16[16,128,512]{2,1,0:T(8,128)(2,1)S(1)} custom-call(s32[8,16]{1,0:T(8,128)} %bitcast.8, s32[1,4]{1,0:T(1,128)} %order_hbm.1, bf16[16,128,512]{2,1,0:T(8,128)(2,1)} %bitcast.6, bf16[16,8,128,128]{3,2,1,0:T(8,128)(2,1)} %adj_hbm.1, bf16[512,512]{1,0:T(8,128)(2,1)} %bitcast.7), custom_call_target="tpu_custom_call" | custom-call | tf_op jit(solution)/shard_map/pallas_call | solution.py:594
  113.1 0.0 copy-done
  113.1 1.9 %shard_map.56 = bf16[16,128,512]{2,1,0:T(8,128)(2,1)} custom-call(s32[4]{0:T(128)S(1)} %bitcast.5, bf16[16,128,512]{2,1,0:T(8,128)(2,1)S(1)} %shard_map.55.h_ref), custom_call_target="tpu_custom_call" | custom-call | tf_op jit(solution)/shard_map/pallas_call | solution.py:645
Async XLA Ops:
  0.0 113.1 %copy-start = (s32[1,4]{1,0:T(1,128)S(1)}, s32[1,4]{1,0:T(1,128)}, u32[]{:S(2)}) copy-start(s32[1,4]{1,0:T(1,128)} %order_hbm.1) | copy-start | bytes 52

commit v7 on v6

--- a/solution.py
+++ b/solution.py
@@ -10,7 +10,7 @@
 MESH = pl.DeviceIdType.MESH
 SPLIT = 2
 UP = 4
-AHEAD = 4
+AHEAD = 3
 FIRST_AHEAD = 0
 RUN = 2
 LAG = 4

time: 116 us -> 116 us (level)
  no operation moved by 1% of the time
where the time goes in v7:
time: 116 us
  Pallas kernels  116 us (100%)
    pallas_call x1, Pallas kernels, on_device(): pl.pallas_call(functools.partial(pipeline_kernel, sections, parts, groups...  114 us

profile of v7, /device:TPU:27, one launch (start us, length us, event | category | flops | bytes accessed | tf_op | source)
XLA Modules:
  0.0 115.7 jit_solution(11903798625692598311)
XLA Ops:
  0.0 0.0 copy-start
  0.0 113.8 %shard_map.55.h_ref = bf16[16,128,512]{2,1,0:T(8,128)(2,1)S(1)} custom-call(s32[8,16]{1,0:T(8,128)} %bitcast.8, s32[1,4]{1,0:T(1,128)} %order_hbm.1, bf16[16,128,512]{2,1,0:T(8,128)(2,1)} %bitcast.6, bf16[16,8,128,128]{3,2,1,0:T(8,128)(2,1)} %adj_hbm.1, bf16[512,512]{1,0:T(8,128)(2,1)} %bitcast.7), custom_call_target="tpu_custom_call" | custom-call | tf_op jit(solution)/shard_map/pallas_call | solution.py:594
  113.8 0.0 copy-done
  113.8 1.9 %shard_map.56 = bf16[16,128,512]{2,1,0:T(8,128)(2,1)} custom-call(s32[4]{0:T(128)S(1)} %bitcast.5, bf16[16,128,512]{2,1,0:T(8,128)(2,1)S(1)} %shard_map.55.h_ref), custom_call_target="tpu_custom_call" | custom-call | tf_op jit(solution)/shard_map/pallas_call | solution.py:645
Async XLA Ops:
  0.0 113.8 %copy-start = (s32[1,4]{1,0:T(1,128)S(1)}, s32[1,4]{1,0:T(1,128)}, u32[]{:S(2)}) copy-start(s32[1,4]{1,0:T(1,128)} %order_hbm.1) | copy-start | bytes 52
